TPU v7x, 32 devices: a whole 2x2x4 slice. The times are simulated.
32 devices in a mesh: section: 4 (over x, core), tensor: 2 (over y), dp: 4 (over z).
Axes of the slice: x: 2, y: 2, z: 4, core: 2. Of those that a mesh axis runs over, the one named last changes fastest.
Arguments:
- residuals: bfloat16 [4, 4, 2, 128, 8192], P('section', 'dp', None, 'tensor'), may hold values from -6 to 6
- norm_gain: bfloat16 [4, 8192], P('section'), may hold values from 0.5 to 1.5
- projection: bfloat16 [4, 8192, 2, 2, 128], P('section', None, 'tensor'), may hold values from -0.0625 to 0.0625
- queries: bfloat16 [4, 4, 2, 128, 2, 1024], P('section', 'dp', None, None, 'tensor'), may hold values from -48 to 48
- output_grad: bfloat16 [4, 4, 2, 128, 2, 1024], P('section', 'dp', None, None, 'tensor'), may hold values from -6 to 6
- section_cotangent: bfloat16 [4, 4, 128, 8192], P('section', 'dp', 'tensor'), may hold values from -6 to 6
- loss_cotangent: bfloat16 [4, 128, 8192], P('dp', 'tensor'), may hold values from -6 to 6
- lengths: int32 [4, 4, 2], P('section', 'dp'), may hold values from 64 to 128
- segments: int32 [4, 4, 2, 128], P('section', 'dp'), may hold values from 0 to 2, never falling along the last dimension, each value on 1 to 64 neighbouring positions
Outputs:
- query_grad: bfloat16 [4, 4, 2, 128, 2, 1024], P('section', 'dp', None, None, 'tensor')
- residual_grad: bfloat16 [4, 4, 128, 8192], P('section', 'dp', 'tensor')
- projection_grad: bfloat16 [4, 8192, 2, 2, 128], P('section', 'dp', 'tensor')
All inputs are finite; a program needn't handle non-finite values.
Results may differ from a plain program's by a relative error of at most 0.015.
Values may be sent and summed in bfloat16 or wider, within the bound.
A program may use at most 64 MiB of HBM per device.

v0:
```python
import jax
import jax.numpy as jnp
from jax import lax
from jax.sharding import PartitionSpec as P


EPSILON = 1e-05
MASKED = -1e30


def shifted(value, axis, steps):
    count = lax.axis_size(axis)
    leading, last = (max(0, -steps), min(count, count - steps))
    return lax.ppermute(value, axis, [(source, source + steps) for source in range(leading, last)])


def normalize(residual, gain_wide):
    upcast = residual.astype(jnp.float32)
    inverse = lax.rsqrt(jnp.mean(upcast * upcast, axis=-1, keepdims=True) + EPSILON)
    return ((upcast * inverse * gain_wide).astype(jnp.bfloat16), inverse)


def project(rows, weights):
    return jnp.dot(rows, weights, preferred_element_type=jnp.float32).astype(jnp.bfloat16)


def head_grads(projected, query_rows, grad_rows, length, segment):
    head_size = projected.shape[1] // 2
    row_total = projected.shape[0]
    group_size = query_rows.shape[-1] // head_size
    scaling = head_size ** (-0.5)
    key_rows = projected[:, :head_size]
    value_rows = projected[:, head_size:]
    position = lax.iota(jnp.int32, row_total)
    visible = (position[None, :] <= position[:, None]) & (segment[:, None] == segment[None, :])
    live_mask = (position < length).astype(jnp.bfloat16)
    query = query_rows.reshape(row_total, group_size, head_size)
    masked_grad = grad_rows.reshape(row_total, group_size, head_size) * live_mask[:, None, None]
    scores = (
        jnp.einsum("qgd,kd->gqk", query, key_rows, preferred_element_type=jnp.float32) * scaling
    )
    scores = jnp.where(visible[None], scores, MASKED)
    row_max = jnp.max(scores, axis=-1, keepdims=True)
    exponent = jnp.exp(scores - row_max)
    attention = exponent / jnp.sum(exponent, axis=-1, keepdims=True)
    attention_low = attention.astype(jnp.bfloat16)
    mixed = jnp.einsum("gqk,kd->gqd", attention_low, value_rows, preferred_element_type=jnp.float32)
    correction = jnp.sum(mixed * jnp.transpose(masked_grad, (1, 0, 2)).astype(jnp.float32), axis=-1)
    value_grad = jnp.einsum(
        "gqk,qgd->kd", attention_low, masked_grad, preferred_element_type=jnp.float32
    )
    weight_grad = jnp.einsum(
        "qgd,kd->gqk", masked_grad, value_rows, preferred_element_type=jnp.float32
    )
    score_grad = (attention * (weight_grad - correction[..., None])).astype(jnp.bfloat16)
    query_grad = (
        jnp.einsum("gqk,kd->qgd", score_grad, key_rows, preferred_element_type=jnp.float32)
        * scaling
    ).astype(jnp.bfloat16)
    key_grad = (
        jnp.einsum("gqk,qgd->kd", score_grad, query, preferred_element_type=jnp.float32) * scaling
    )
    pair_grad = jnp.concatenate([key_grad, value_grad], axis=1).astype(jnp.bfloat16)
    return (query_grad.reshape(row_total, 1, group_size * head_size), pair_grad)


def rotated(value, axis, steps):
    count = lax.axis_size(axis)
    return lax.ppermute(value, axis, [(source, (source + steps) % count) for source in range(count)])


def after(value, *earlier):
    return lax.optimization_barrier((value, *earlier))[0]


def on_device(
    residuals,
    norm_gain,
    projection,
    queries,
    output_grad,
    section_cotangent,
    loss_cotangent,
    lengths,
    segments,
):
    local_rows = residuals[0, 0]
    tick_count, row_count, model_width = local_rows.shape
    head_size = projection.shape[4]
    pair_width = 2 * head_size
    weights = projection.reshape(model_width, pair_width)
    gain_wide = norm_gain[0].astype(jnp.float32)
    tensor_count = lax.axis_size("tensor")
    tensor_index = lax.axis_index("tensor")
    dp_count = lax.axis_size("dp")
    dp_index = lax.axis_index("dp")
    block_width = model_width // dp_count
    row_total = row_count * tensor_count
    ticks = range(tick_count)

    def owner_start(steps):
        return lax.rem(tensor_index + (tensor_count + steps), tensor_count) * row_count

    def column_block(value, steps):
        start = lax.rem(dp_index + steps, dp_count) * block_width
        return lax.dynamic_slice_in_dim(value, start, block_width, axis=value.ndim - 1)

    normed_ticks, inverse_ticks, arrived = [], [], []
    for tick in ticks:
        rows = after(local_rows[tick], *normed_ticks)
        normed, inverse = normalize(rows, gain_wide)
        normed_ticks.append(normed)
        inverse_ticks.append(inverse)
        arrived.append([rotated(normed, "tensor", k) for k in range(1, tensor_count)])
    normed_local = jnp.stack(normed_ticks)

    own_columns = [column_block(normed_local, 0)] + [
        rotated(column_block(normed_local, j), "dp", j) for j in range(1, dp_count)
    ]

    projected_own = project(normed_local.reshape(-1, model_width), weights)
    projected_own = projected_own.reshape(tick_count, row_count, pair_width)

    query_list, pair_list, received, kept = [], [], [], []
    other_ticks = []
    sent = ()
    for tick in ticks:
        gathered = after(arrived[tick], *sent)
        columns = [
            [column_block(rows, j) for rows in gathered] for j in range(dp_count)
        ]
        columns = lax.optimization_barrier(columns)
        if tick > 0:
            gathered = after(gathered, columns)
        pieces = [projected_own[tick]] + [project(rows, weights) for rows in gathered]
        projected = jnp.zeros((row_total, pair_width), jnp.bfloat16)
        for k, piece in enumerate(pieces):
            projected = lax.dynamic_update_slice_in_dim(
                projected, piece, owner_start(-k), axis=0
            )
        query_grad, pair_grad = head_grads(
            projected,
            queries[0, 0, tick],
            output_grad[0, 0, tick],
            lengths[0, 0, tick],
            segments[0, 0, tick],
        )

        def partial(pairs, steps):
            rows = lax.dynamic_slice_in_dim(pairs, owner_start(steps), row_count, axis=0)
            return lax.dot_general(
                rows, weights, (((1,), (1,)), ((), ())), preferred_element_type=jnp.float32
            ).astype(jnp.bfloat16)

        leaving = [partial(pair_grad, k) for k in range(1, tensor_count)]
        leaving = lax.optimization_barrier(leaving)
        received.append([rotated(value, "tensor", k + 1) for k, value in enumerate(leaving)])
        sent = tuple(leaving)
        query_grad, pair_grad = after((query_grad, pair_grad), *sent)
        if tick == 0:
            columns = after(columns, *sent)
        other_ticks.append(
            [columns[0]]
            + [[rotated(value, "dp", j) for value in columns[j]] for j in range(1, dp_count)]
        )
        query_list.append(query_grad)
        kept.append(partial(pair_grad, 0))
        pair_list.append(
            jnp.stack(
                [
                    lax.dynamic_slice_in_dim(pair_grad, owner_start(-k), row_count, axis=0)
                    for k in range(tensor_count)
                ]
            )
        )

    pair_local = jnp.stack(pair_list, axis=1)
    pair_all = [pair_local] + [rotated(pair_local, "dp", j) for j in range(1, dp_count)]

    def norm_back(tick, *earlier):
        normed_grad = kept[tick].astype(jnp.float32)
        for part in after(received[tick], *earlier):
            normed_grad = normed_grad + part.astype(jnp.float32)
        upcast = local_rows[tick].astype(jnp.float32)
        inverse = inverse_ticks[tick]
        scaled = normed_grad * gain_wide
        return inverse * scaled - upcast * inverse * inverse * inverse * jnp.mean(
            scaled * upcast, axis=-1, keepdims=True
        )

    outgoing = section_cotangent[0, 0].astype(jnp.float32) + norm_back(0)
    outgoing = outgoing.astype(jnp.bfloat16)
    incoming = shifted(outgoing, "section", -1)
    is_last = lax.axis_index("section") == lax.axis_size("section") - 1
    incoming = jnp.where(is_last, loss_cotangent[0], incoming)
    residual_grad = (incoming.astype(jnp.float32) + norm_back(1, outgoing)).astype(jnp.bfloat16)

    own_columns, other_ticks, pair_all = after((own_columns, other_ticks, pair_all), outgoing)

    def contract(columns, pairs):
        left = jnp.concatenate([value.reshape(-1, block_width) for value in columns])
        right = jnp.concatenate([value.reshape(-1, pair_width) for value in pairs])
        return lax.dot_general(
            left, right, (((0,), (0,)), ((), ())), preferred_element_type=jnp.float32
        )

    weight_sum = contract(own_columns, [value[0] for value in pair_all])
    if tensor_count > 1:
        others = [
            jnp.stack([jnp.stack([other_ticks[tick][j][k] for tick in ticks]) for k in range(tensor_count - 1)])
            for j in range(dp_count)
        ]
        weight_sum = weight_sum + contract(others, [value[1:] for value in pair_all])
    projection_grad = weight_sum.astype(jnp.bfloat16).reshape(1, -1, 1, 2, head_size)
    query_all = jnp.stack(query_list)[None, None]
    return (query_all, residual_grad[None, None], projection_grad)


def solution(mesh):
    in_specs = (
        P("section", "dp", None, "tensor", None),
        P("section", None),
        P("section", None, "tensor", None, None),
        P("section", "dp", None, None, "tensor", None),
        P("section", "dp", None, None, "tensor", None),
        P("section", "dp", "tensor", None),
        P("dp", "tensor", None),
        P("section", "dp", None),
        P("section", "dp", None, None),
    )
    out_specs = (
        P("section", "dp", None, None, "tensor", None),
        P("section", "dp", "tensor", None),
        P("section", "dp", "tensor", None, None),
    )


    return jax.shard_map(on_device, mesh=mesh, in_specs=in_specs, out_specs=out_specs, check_vma=False)
```

profile of v0, /device:TPU:0, one launch (start us, length us, event | category | flops | bytes accessed | tf_op | source)
XLA Modules:
  0.0 156.5 jit_solution(17524337425583165910)
XLA Ops:
  0.6 0.8 mul.265
  1.4 1.7 %slice_bitcast_fusion.1 = (bf16[64,8192]{1,0:T(8,128)(2,1)S(1)}, bf16[64,8192]{1,0:T(8,128)(2,1)S(1)}) fusion(bf16[1,1,2,64,8192]{4,3,2,1,0:T(8,128)(2,1)} %param.9), kind=kLoop, calls=%fused_computation.124 | loop fusion | bytes 4194304 | tf_op jit(solution)/shard_map/squeeze | solution.py:110
  3.4 1.3 fusion.17
  4.7 3.0 %collective-permute-start = (bf16[64,8192]{1,0:T(8,128)(2,1)}, bf16[64,8192]{1,0:T(8,128)(2,1)}, u32[]{:S(2)}, u32[]{:S(2)}) collective-permute-start(bf16[64,8192]{1,0:T(8,128)(2,1)} %fusion.17), channel_id=1, source_target_pairs={{0,4},{4,0},{1,5},{5,1},{2,6},{6,2},{3,7},{7,3},{8,12},{12,8},{9,1... | collective-permute-start | bytes 3145736 | tf_op jit(solution)/shard_map/ppermute | solution.py:69
  8.0 1.3 fusion.20
  10.0 1.4 fusion.100
  11.3 4.1 %collective-permute-start.7 = (bf16[2,64,2048]{2,1,0:T(8,128)(2,1)}, bf16[2,64,2048]{2,1,0:T(8,128)(2,1)}, u32[]{:S(2)}, u32[]{:S(2)}) collective-permute-start(bf16[2,64,2048]{2,1,0:T(8,128)(2,1)} %get-tuple-element.84), channel_id=1, source_target_pairs={{0,3},{1,0},{2,1},{3,2},{4,7},{5,4},{6,5},{7,6},{8,11},{9,8},{10,9... | collective-permute-start | bytes 1572872 | tf_op jit(solution)/shard_map/ppermute | solution.py:69
  15.4 1.1 collective-permute-start.6
  16.5 1.5 pad_maximum_fusion
  21.2 3.1 %fusion.75 = bf16[128,256]{1,0:T(8,128)(2,1)S(1)} fusion(bf16[128,8192]{1,0:T(8,128)(2,1)S(1)} %bitcast.303, bf16[1024,8,2,128]{3,2,1,0:T(2,128)(2,1)} %bitcast.282), kind=kOutput, calls=%fused_computation.107 | convolution fusion | flops 536903680 | bytes 6356992 | tf_op jit(solution)/shard_map/dot_general | solution.py:24
  24.3 7.7 %collective-permute-done = bf16[64,8192]{1,0:T(8,128)(2,1)} collective-permute-done((bf16[64,8192]{1,0:T(8,128)(2,1)}, bf16[64,8192]{1,0:T(8,128)(2,1)}, u32[]{:S(2)}, u32[]{:S(2)}) %collective-permute-start) | collective-permute-done | bytes 1048608 | tf_op jit(solution)/shard_map/ppermute | solution.py:69
  32.0 2.1 %fusion.93 = bf16[128,256]{1,0:T(8,128)(2,1)S(1)} fusion(bf16[128,256]{1,0:T(8,128)(2,1)S(1)} %slice_dynamic-update-slice_fusion.1, s32[]{:T(128)S(6)} %select_n.54, bf16[64,8192]{1,0:T(8,128)(2,1)} %collective-permute-done, bf16[1024,8,2,128]{3,2,1,0:T(2,128)(2,1)S(1)} %bitcast.287), kind=kOutput, calls=%fused_computation.121 | convolution fusion | flops 268451840 | bytes 5275652 | tf_op jit(solution)/shard_map/dot_general | solution.py:24
  35.5 4.6 %convolution_convert_fusion.3 = bf16[64,8192]{1,0:T(8,128)(2,1)} fusion(bf16[1024,8,2,128]{3,2,1,0:T(2,128)(2,1)} %bitcast.283, s32[]{:T(128)S(6)} %select_n.56, bf16[128,128]{0,1:T(8,128)(2,1)S(1)} %fusion.88, bf16[128,128]{0,1:T(8,128)(2,1)S(1)} %fusion.80), kind=kOutput, calls=%fused_computation.7 | convolution fusion | flops 269025280 | bytes 5308420 | tf_op jit(solution)/shard_map/dot_general | solution.py:151
  40.4 13.2 %collective-permute-done.1 = bf16[64,8192]{1,0:T(8,128)(2,1)} collective-permute-done((bf16[64,8192]{1,0:T(8,128)(2,1)}, bf16[64,8192]{1,0:T(8,128)(2,1)}, u32[]{:S(2)}, u32[]{:S(2)}) %collective-permute-start.1) | collective-permute-done | bytes 1048608 | tf_op jit(solution)/shard_map/ppermute | solution.py:69
  53.6 2.8 %constant_dynamic-slice_fusion.2 = (bf16[64,2048]{1,0:T(8,128)(2,1)}, bf16[64,2048]{1,0:T(8,128)(2,1)}, bf16[64,2048]{1,0:T(8,128)(2,1)}, bf16[64,2048]{1,0:T(8,...) fusion(bf16[64,8192]{1,0:T(8,128)(2,1)} %collective-permute-don, ...), kind=kLoop, calls=%fused_computation.191 | loop fusion | bytes 4194320 | tf_op jit(solution)/shard_map/dynamic_slice | solution.py:106
  56.5 2.1 %fusion.90 = bf16[128,256]{1,0:T(8,128)(2,1)S(1)} fusion(bf16[128,256]{1,0:T(8,128)(2,1)S(1)} %slice_dynamic-update-slice_fusion, s32[]{:T(128)S(6)} %select_n.54, bf16[64,8192]{1,0:T(8,128)(2,1)} %collective-permute-done.1, bf16[1024,8,2,128]{3,2,1,0:T(2,128)(2,1)S(1)} %bitcast.288), kind=kOutput, calls=%fused_computation.120 | convolution fusion | flops 268451840 | bytes 5275652 | tf_op jit(solution)/shard_map/dot_general | solution.py:24
  59.5 1.8 %collective-permute-start.2 = (bf16[64,8192]{1,0:T(8,128)(2,1)}, bf16[64,8192]{1,0:T(8,128)(2,1)}, u32[]{:S(2)}, u32[]{:S(2)}) collective-permute-start(bf16[64,8192]{1,0:T(8,128)(2,1)} %convolution_convert_fusion.3), channel_id=1, source_target_pairs={{0,4},{4,0},{1,5},{5,1},{2,6},{6,2},{3,7},{7,3},{8,12},{12,8},{9,1... | collective-permute-start | bytes 3145736 | tf_op jit(solution)/shard_map/ppermute | solution.py:69
  61.3 0.9 copy.66
  62.7 4.6 %convolution_convert_fusion.2 = bf16[64,8192]{1,0:T(8,128)(2,1)} fusion(bf16[1024,8,2,128]{3,2,1,0:T(2,128)(2,1)} %bitcast.284, s32[]{:T(128)S(6)} %select_n.56, bf16[128,128]{0,1:T(8,128)(2,1)S(1)} %fusion.89, bf16[128,128]{0,1:T(8,128)(2,1)S(1)} %fusion.81), kind=kOutput, calls=%fused_computation.6 | convolution fusion | flops 269025280 | bytes 5308420 | tf_op jit(solution)/shard_map/dot_general | solution.py:151
  69.7 1.7 %fusion.72 = bf16[128,8,128]{2,0,1:T(8,128)(2,1)} fusion(bf16[8,128,128]{1,2,0:T(8,128)(2,1)S(1)} %fusion.69, bf16[128,256]{1,0:T(8,128)(2,1)} %copy-done.12), kind=kOutput, calls=%fused_computation.104 | convolution fusion | flops 33816576 | bytes 557056 | tf_op jit(solution)/shard_map/gqk,kd->qgd/dot_general | solution.py:57
  71.4 1.1 copy.77
  72.5 1.6 %constant_dynamic-slice_fusion = (bf16[64,256]{0,1:T(8,128)(2,1)}, bf16[64,256]{0,1:T(8,128)(2,1)S(1)}) fusion(bf16[128,256]{0,1:T(8,128)(2,1)} %pad_maximum_fusion.7, s32[]{:T(128)S(6)} %select_n.54, s32[]{:T(128)S(6)} %select_n.27), kind=kLoop, calls=%fused_computation.189 | loop fusion | bytes 131080 | tf_op jit(solution)/shard_map/dynamic_slice | solution.py:171
  74.1 1.5 copy.81
  77.1 0.8 maximum_bitcast_fusion.2
  77.9 1.8 %maximum_bitcast_fusion = bf16[1,1,2,128,1,1024]{5,3,4,2,1,0:T(8,128)(2,1)} fusion(bf16[1,128,1,1024]{3,1,0,2:T(8,128)(2,1)S(1)} %bitcast.312, bf16[1,128,1,1024]{3,1,0,2:T(8,128)(2,1)} %bitcast.311), kind=kLoop, calls=%fused_computation.130 | loop fusion | flops 262144 | bytes 1048576 | tf_op jit(solution)/shard_map/broadcast_in_dim | solution.py:215
  79.8 6.2 %collective-permute-done.2 = bf16[64,8192]{1,0:T(8,128)(2,1)} collective-permute-done((bf16[64,8192]{1,0:T(8,128)(2,1)}, bf16[64,8192]{1,0:T(8,128)(2,1)}, u32[]{:S(2)}, u32[]{:S(2)}) %collective-permute-start.2) | collective-permute-done | bytes 1048608 | tf_op jit(solution)/shard_map/ppermute | solution.py:69
  85.9 1.8 %collective-permute-start.11 = (bf16[64,2048]{1,0:T(8,128)(2,1)}, bf16[64,2048]{1,0:T(8,128)(2,1)S(1)}, u32[]{:S(2)}, u32[]{:S(2)}) collective-permute-start(bf16[64,2048]{1,0:T(8,128)(2,1)} %get-tuple-element.43), channel_id=1, source_target_pairs={{0,1},{1,2},{2,3},{3,0},{4,5},{5,6},{6,7},{7,4},{8,9},{9,10},{10,1... | collective-permute-start | bytes 786440 | tf_op jit(solution)/shard_map/ppermute | solution.py:69
  87.7 4.1 %fusion.27 = (f32[64]{0:T(128)S(1)}, f32[64,8192]{1,0:T(8,128)S(1)}) fusion(bf16[64,8192]{1,0:T(8,128)(2,1)} %collective-permute-done.2, f32[8192]{0:T(1024)S(1)} %bitcast.293, bf16[1,1,2,64,8192]{4,3,2,1,0:T(8,128)(2,1)S(1)} %copy-done.2, bf16[64,256]{0,1:T(8,128)(2,1)} %copy-done.8, bf16[1024,8,2,128]{3,2,1,0:T(2,128)(2,1)} %bitcast.285), kind=kOutput, calls=%fused_computation.49 | convolution fusion | flops 272629696 | bytes 8454400 | tf_op jit(solution)/shard_map/dot_general | solution.py:151
  91.8 2.1 %collective-permute-start.16 = (bf16[2,2,64,256]{3,2,0,1:T(8,128)(2,1)S(1)}, bf16[2,2,64,256]{3,2,0,1:T(8,128)(2,1)S(1)}, u32[]{:S(2)}, u32[]{:S(2)}) collective-permute-start(bf16[2,2,64,256]{3,2,0,1:T(8,128)(2,1)S(1)} %pad_maximum_fusion.5), channel_id=1, source_target_pairs={{0,3},{1,0},{2,1},{3,2},{4,7},{5,4},{6,5},{7,6},{8,11},{9,8},{10,9... | collective-permute-start | bytes 393224 | tf_op jit(solution)/shard_map/ppermute | solution.py:69
  93.9 1.0 collective-permute-start.15
  94.9 1.6 %collective-permute-start.14 = (bf16[2,2,64,256]{3,2,0,1:T(8,128)(2,1)S(1)}, bf16[2,2,64,256]{3,2,0,1:T(8,128)(2,1)S(1)}, u32[]{:S(2)}, u32[]{:S(2)}) collective-permute-start(bf16[2,2,64,256]{3,2,0,1:T(8,128)(2,1)S(1)} %pad_maximum_fusion.5), channel_id=1, source_target_pairs={{0,1},{1,2},{2,3},{3,0},{4,5},{5,6},{6,7},{7,4},{8,9},{9,10},{10,1... | collective-permute-start | bytes 393224 | tf_op jit(solution)/shard_map/ppermute | solution.py:69
  96.5 1.5 collective-permute-done.16
  98.0 8.5 %collective-permute-start.12 = (bf16[64,2048]{1,0:T(8,128)(2,1)S(1)}, bf16[64,2048]{1,0:T(8,128)(2,1)S(1)}, u32[]{:S(2)}, u32[]{:S(2)}) collective-permute-start(bf16[64,2048]{1,0:T(8,128)(2,1)S(1)} %copy-done.17), channel_id=1, source_target_pairs={{0,2},{1,3},{2,0},{3,1},{4,6},{5,7},{6,4},{7,5},{8,10},{9,11},{10,... | collective-permute-start | bytes 786440 | tf_op jit(solution)/shard_map/ppermute | solution.py:69
  106.5 3.3 %collective-permute-done.15 = bf16[2,2,64,256]{3,2,0,1:T(8,128)(2,1)S(1)} collective-permute-done((bf16[2,2,64,256]{3,2,0,1:T(8,128)(2,1)S(1)}, bf16[2,2,64,256]{3,2,0,1:T(8,128)(2,1)S(1)}, u32[]{:S(2)}, u32[]{:S(2)}) %collective-permute-start.15) | collective-permute-done | bytes 131104 | tf_op jit(solution)/shard_map/ppermute | solution.py:69
  109.9 3.8 %collective-permute-start.8 = (bf16[64,2048]{1,0:T(8,128)(2,1)S(1)}, bf16[64,2048]{1,0:T(8,128)(2,1)S(1)}, u32[]{:S(2)}, u32[]{:S(2)}) collective-permute-start(bf16[64,2048]{1,0:T(8,128)(2,1)S(1)} %copy-done.15), channel_id=1, source_target_pairs={{0,1},{1,2},{2,3},{3,0},{4,5},{5,6},{6,7},{7,4},{8,9},{9,10},{10,1... | collective-permute-start | bytes 786440 | tf_op jit(solution)/shard_map/ppermute | solution.py:69
  113.7 2.5 %collective-permute-start.9 = (bf16[64,2048]{1,0:T(8,128)(2,1)S(1)}, bf16[64,2048]{1,0:T(8,128)(2,1)S(1)}, u32[]{:S(2)}, u32[]{:S(2)}) collective-permute-start(bf16[64,2048]{1,0:T(8,128)(2,1)S(1)} %copy-done.14), channel_id=1, source_target_pairs={{0,2},{1,3},{2,0},{3,1},{4,6},{5,7},{6,4},{7,5},{8,10},{9,11},{10,... | collective-permute-start | bytes 786440 | tf_op jit(solution)/shard_map/ppermute | solution.py:69
  116.1 2.8 %collective-permute-start.10 = (bf16[64,2048]{1,0:T(8,128)(2,1)S(1)}, bf16[64,2048]{1,0:T(8,128)(2,1)S(1)}, u32[]{:S(2)}, u32[]{:S(2)}) collective-permute-start(bf16[64,2048]{1,0:T(8,128)(2,1)S(1)} %copy-done.13), channel_id=1, source_target_pairs={{0,3},{1,0},{2,1},{3,2},{4,7},{5,4},{6,5},{7,6},{8,11},{9,8},{10,9... | collective-permute-start | bytes 786440 | tf_op jit(solution)/shard_map/ppermute | solution.py:69
  119.0 3.1 %fusion.26 = bf16[64,8192]{1,0:T(8,128)(2,1)} fusion(f32[64,8192]{1,0:T(8,128)S(1)} %get-tuple-element.123, bf16[64,8192]{1,0:T(8,128)(2,1)} %collective-permute-done.2, bf16[1,1,64,8192]{3,2,1,0:T(8,128)(2,1)S(1)} %copy-done.4, f32[64]{0:T(128)S(1)} %broadcast_multiply_fusion.13, f32[8192]{0:T(1024)S(1)} %bitcast.294, f32[64]{0:T(128)S(1)} %add_rsqrt_fusion.1, ...), kind=kLoop, calls=%fused_computation.48 | loop fusion | flops 6815744 | bytes 6324736 | tf_op jit(solution)/shard_map/convert_element_type | solution.py:192
  122.1 2.8 %collective-permute-done.12 = bf16[64,2048]{1,0:T(8,128)(2,1)S(1)} collective-permute-done((bf16[64,2048]{1,0:T(8,128)(2,1)S(1)}, bf16[64,2048]{1,0:T(8,128)(2,1)S(1)}, u32[]{:S(2)}, u32[]{:S(2)}) %collective-permute-start.12) | collective-permute-done | bytes 262176 | tf_op jit(solution)/shard_map/ppermute | solution.py:69
  125.0 1.3 collective-permute-start.3
  126.3 1.8 %collective-permute-done.8 = bf16[64,2048]{1,0:T(8,128)(2,1)S(1)} collective-permute-done((bf16[64,2048]{1,0:T(8,128)(2,1)S(1)}, bf16[64,2048]{1,0:T(8,128)(2,1)S(1)}, u32[]{:S(2)}, u32[]{:S(2)}) %collective-permute-start.8) | collective-permute-done | bytes 262176 | tf_op jit(solution)/shard_map/ppermute | solution.py:69
  128.1 12.6 %collective-permute-done.9 = bf16[64,2048]{1,0:T(8,128)(2,1)S(1)} collective-permute-done((bf16[64,2048]{1,0:T(8,128)(2,1)S(1)}, bf16[64,2048]{1,0:T(8,128)(2,1)S(1)}, u32[]{:S(2)}, u32[]{:S(2)}) %collective-permute-start.9) | collective-permute-done | bytes 262176 | tf_op jit(solution)/shard_map/ppermute | solution.py:69
  141.0 0.8 copy-done.11
  141.8 2.1 %fusion.35 = f32[2048,256]{0,1:T(8,128)S(1)} fusion(bf16[128,2048]{1,0:T(8,128)(2,1)} %bitcast.51, bf16[128,2048]{1,0:T(8,128)(2,1)} %bitcast.50, bf16[128,2048]{1,0:T(8,128)(2,1)} %bitcast.49, bf16[128,2048]{1,0:T(8,128)(2,1)S(1)} %bitcast.319, bf16[128,256]{1,0:T(8,128)(2,1)S(1)} %bitcast.337, bf16[128,256]{1,0:T(8,128)(2,1)S(1)} %bitcast.336, ...), kind=kOutput, calls=%fused_computation.57 | convolution fusion | flops 546308096 | bytes 4456448 | tf_op jit(solution)/shard_map/dot_general | solution.py:203
  144.0 1.8 %fusion.14 = bf16[2048,256]{0,1:T(8,128)(2,1)} fusion(f32[2048,256]{0,1:T(8,128)S(1)} %fusion.35, bf16[128,2048]{1,0:T(8,128)(2,1)S(1)} %bitcast.318, bf16[128,2048]{1,0:T(8,128)(2,1)S(1)} %bitcast.317, bf16[128,2048]{1,0:T(8,128)(2,1)S(1)} %bitcast.316, bf16[128,2048]{1,0:T(8,128)(2,1)S(1)} %bitcast.315, bf16[128,256]{1,0:T(8,128)(2,1)S(1)} %bitcast.334, ...), kind=kOutput, calls=%fused_computation.36 | convolution fusion | flops 547356672 | bytes 5505024 | tf_op jit(solution)/shard_map/dot_general | solution.py:203
  145.7 3.7 %copy.82 = bf16[1,2048,1,2,128]{4,3,2,1,0:T(2,128)(2,1)} copy(bf16[1,2048,1,2,128]{1,4,3,2,0:T(8,128)(2,1)} %bitcast.304) | data formatting | bytes 2097152
  149.4 3.8 %fusion.34 = (f32[64]{0:T(128)S(1)}, f32[64,8192]{1,0:T(8,128)S(1)}) fusion(bf16[64,8192]{1,0:T(8,128)(2,1)S(1)} %collective-permute-done.4, f32[8192]{0:T(1024)S(1)} %bitcast.295, bf16[1,1,2,64,8192]{4,3,2,1,0:T(8,128)(2,1)S(1)} %copy-done.2, bf16[64,256]{0,1:T(8,128)(2,1)S(1)} %get-tuple-element.113, bf16[1024,8,2,128]{3,2,1,0:T(2,128)(2,1)} %bitcast.286), kind=kOutput, calls=%fused_computation.56 | convolution fusion | flops 272629696 | bytes 8454400 | tf_op jit(solution)/shard_map/dot_general | solution.py:151
  153.3 3.2 %fusion.96 = bf16[1,1,64,8192]{3,2,1,0:T(8,128)(2,1)} fusion(f32[64]{0:T(128)S(1)} %broadcast_multiply_fusion.12, f32[8192]{0:T(1024)S(1)} %bitcast.296, f32[64,8192]{1,0:T(8,128)S(1)} %get-tuple-element.125, bf16[64,8192]{1,0:T(8,128)(2,1)S(1)} %collective-permute-done.4, f32[64]{0:T(128)S(1)} %add_rsqrt_fusion, ...), kind=kLoop, calls=%fused_computation.125 | loop fusion | flops 7340032 | bytes 7373313 | tf_op jit(solution)/shard_map/broadcast_in_dim | solution.py:216
  (105 shorter events, 11.4 us)
Async XLA Ops:
  4.7 27.3 %collective-permute-start = (bf16[64,8192]{1,0:T(8,128)(2,1)}, bf16[64,8192]{1,0:T(8,128)(2,1)}, u32[]{:S(2)}, u32[]{:S(2)}) collective-permute-start(bf16[64,8192]{1,0:T(8,128)(2,1)} %fusion.17), channel_id=1, source_target_pairs={{0,4},{4,0},{1,5},{5,1},{2,6},{6,2},{3,7},{7,3},{8,12},{12,8},{9,1... | collective-permute-start | bytes 3145736 | tf_op jit(solution)/shard_map/ppermute | solution.py:69
  9.3 44.3 %collective-permute-start.1 = (bf16[64,8192]{1,0:T(8,128)(2,1)}, bf16[64,8192]{1,0:T(8,128)(2,1)}, u32[]{:S(2)}, u32[]{:S(2)}) collective-permute-start(bf16[64,8192]{1,0:T(8,128)(2,1)} %fusion.20), channel_id=1, source_target_pairs={{0,4},{4,0},{1,5},{5,1},{2,6},{6,2},{3,7},{7,3},{8,12},{12,8},{9,1... | collective-permute-start | bytes 3145736 | tf_op jit(solution)/shard_map/ppermute | solution.py:69
  11.3 80.5 %collective-permute-start.7 = (bf16[2,64,2048]{2,1,0:T(8,128)(2,1)}, bf16[2,64,2048]{2,1,0:T(8,128)(2,1)}, u32[]{:S(2)}, u32[]{:S(2)}) collective-permute-start(bf16[2,64,2048]{2,1,0:T(8,128)(2,1)} %get-tuple-element.84), channel_id=1, source_target_pairs={{0,3},{1,0},{2,1},{3,2},{4,7},{5,4},{6,5},{7,6},{8,11},{9,8},{10,9... | collective-permute-start | bytes 1572872 | tf_op jit(solution)/shard_map/ppermute | solution.py:69
  15.4 78.5 %collective-permute-start.5 = (bf16[2,64,2048]{2,1,0:T(8,128)(2,1)}, bf16[2,64,2048]{2,1,0:T(8,128)(2,1)}, u32[]{:S(2)}, u32[]{:S(2)}) collective-permute-start(bf16[2,64,2048]{2,1,0:T(8,128)(2,1)} %get-tuple-element.86), channel_id=1, source_target_pairs={{0,1},{1,2},{2,3},{3,0},{4,5},{5,6},{6,7},{7,4},{8,9},{9,10},{10,1... | collective-permute-start | bytes 1572872 | tf_op jit(solution)/shard_map/ppermute | solution.py:69
  15.4 2.6 %copy-start.18 = (s32[1,1,2]{2,1,0:T(1,128)S(1)}, s32[1,1,2]{2,1,0:T(1,128)}, u32[]{:S(2)}) copy-start(s32[1,1,2]{2,1,0:T(1,128)} %param.16) | copy-start | bytes 28
  15.4 3.2 %copy-start.19 = (s32[1,1,2,128]{3,2,1,0:T(2,128)S(1)}, s32[1,1,2,128]{3,2,1,0:T(2,128)}, u32[]{:S(2)}) copy-start(s32[1,1,2,128]{3,2,1,0:T(2,128)} %param.17) | copy-start | bytes 3076
  15.4 3.4 %copy-start.9 = (bf16[1,1,2,128,1,1024]{5,3,4,2,1,0:T(8,128)(2,1)S(1)}, bf16[1,1,2,128,1,1024]{5,3,4,2,1,0:T(8,128)(2,1)}, u32[]{:S(2)}) copy-start(bf16[1,1,2,128,1,1024]{5,3,4,2,1,0:T(8,128)(2,1)} %param.12) | copy-start | bytes 1572868
  15.4 3.4 %copy-start.10 = (bf16[1,1,2,128,1,1024]{5,3,4,2,1,0:T(8,128)(2,1)S(1)}, bf16[1,1,2,128,1,1024]{5,3,4,2,1,0:T(8,128)(2,1)}, u32[]{:S(2)}) copy-start(bf16[1,1,2,128,1,1024]{5,3,4,2,1,0:T(8,128)(2,1)} %param.13) | copy-start | bytes 1572868
  15.4 79.5 %collective-permute-start.6 = (bf16[2,64,2048]{2,1,0:T(8,128)(2,1)}, bf16[2,64,2048]{2,1,0:T(8,128)(2,1)}, u32[]{:S(2)}, u32[]{:S(2)}) collective-permute-start(bf16[2,64,2048]{2,1,0:T(8,128)(2,1)} %get-tuple-element.87), channel_id=1, source_target_pairs={{0,2},{1,3},{2,0},{3,1},{4,6},{5,7},{6,4},{7,5},{8,10},{9,11},{10,... | collective-permute-start | bytes 1572872 | tf_op jit(solution)/shard_map/ppermute | solution.py:69
  18.8 2.4 %copy-start.3 = (bf16[2,64,8192]{2,1,0:T(8,128)(2,1)S(1)}, bf16[2,64,8192]{2,1,0:T(8,128)(2,1)}, u32[]{:S(2)}) copy-start(bf16[2,64,8192]{2,1,0:T(8,128)(2,1)} %pad_maximum_fusion) | copy-start | bytes 6291460
  21.2 10.9 %copy-start = (bf16[1,8192,1,2,128]{4,3,2,1,0:T(2,128)(2,1)S(1)}, bf16[1,8192,1,2,128]{4,3,2,1,0:T(2,128)(2,1)}, u32[]{:S(2)}) copy-start(bf16[1,8192,1,2,128]{4,3,2,1,0:T(2,128)(2,1)} %param.11) | copy-start | bytes 12582916
  40.4 16.1 %copy-start.1 = (bf16[1,8192,1,2,128]{4,3,2,1,0:T(2,128)(2,1)S(1)}, bf16[1,8192,1,2,128]{4,3,2,1,0:T(2,128)(2,1)}, u32[]{:S(2)}) copy-start(bf16[1,8192,1,2,128]{4,3,2,1,0:T(2,128)(2,1)} %param.11) | copy-start | bytes 12582916
  58.6 3.8 %copy-start.12 = (bf16[128,256]{1,0:T(8,128)(2,1)}, bf16[128,256]{1,0:T(8,128)(2,1)S(1)}, u32[]{:S(2)}) copy-start(bf16[128,256]{1,0:T(8,128)(2,1)S(1)} %fusion.90) | copy-start | bytes 196612
  59.5 26.4 %collective-permute-start.2 = (bf16[64,8192]{1,0:T(8,128)(2,1)}, bf16[64,8192]{1,0:T(8,128)(2,1)}, u32[]{:S(2)}, u32[]{:S(2)}) collective-permute-start(bf16[64,8192]{1,0:T(8,128)(2,1)} %convolution_convert_fusion.3), channel_id=1, source_target_pairs={{0,4},{4,0},{1,5},{5,1},{2,6},{6,2},{3,7},{7,3},{8,12},{12,8},{9,1... | collective-permute-start | bytes 3145736 | tf_op jit(solution)/shard_map/ppermute | solution.py:69
  67.3 20.4 %copy-start.2 = (bf16[1,1,2,64,8192]{4,3,2,1,0:T(8,128)(2,1)S(1)}, bf16[1,1,2,64,8192]{4,3,2,1,0:T(8,128)(2,1)}, u32[]{:S(2)}) copy-start(bf16[1,1,2,64,8192]{4,3,2,1,0:T(8,128)(2,1)} %param.9) | copy-start | bytes 6291460
  67.4 0.6 copy-start.8
  68.7 47.4 %collective-permute-start.4 = (bf16[64,8192]{1,0:T(8,128)(2,1)}, bf16[64,8192]{1,0:T(8,128)(2,1)S(1)}, u32[]{:S(2)}, u32[]{:S(2)}) collective-permute-start(bf16[64,8192]{1,0:T(8,128)(2,1)} %convolution_convert_fusion.2), channel_id=1, source_target_pairs={{0,4},{4,0},{1,5},{5,1},{2,6},{6,2},{3,7},{7,3},{8,12},{12,8},{9,1... | collective-permute-start | bytes 3145736 | tf_op jit(solution)/shard_map/ppermute | solution.py:69
  79.7 18.3 %copy-start.17 = (bf16[64,2048]{1,0:T(8,128)(2,1)S(1)}, bf16[64,2048]{1,0:T(8,128)(2,1)}, u32[]{:S(2)}) copy-start(bf16[64,2048]{1,0:T(8,128)(2,1)} %get-tuple-element.44) | copy-start | bytes 786436
  79.7 30.1 %copy-start.16 = (bf16[64,2048]{1,0:T(8,128)(2,1)S(1)}, bf16[64,2048]{1,0:T(8,128)(2,1)}, u32[]{:S(2)}) copy-start(bf16[64,2048]{1,0:T(8,128)(2,1)} %get-tuple-element.45) | copy-start | bytes 786436
  79.7 30.2 %copy-start.15 = (bf16[64,2048]{1,0:T(8,128)(2,1)S(1)}, bf16[64,2048]{1,0:T(8,128)(2,1)}, u32[]{:S(2)}) copy-start(bf16[64,2048]{1,0:T(8,128)(2,1)} %get-tuple-element.56) | copy-start | bytes 786436
  79.7 33.9 %copy-start.14 = (bf16[64,2048]{1,0:T(8,128)(2,1)S(1)}, bf16[64,2048]{1,0:T(8,128)(2,1)}, u32[]{:S(2)}) copy-start(bf16[64,2048]{1,0:T(8,128)(2,1)} %get-tuple-element.57) | copy-start | bytes 786436
  79.7 36.4 %copy-start.13 = (bf16[64,2048]{1,0:T(8,128)(2,1)S(1)}, bf16[64,2048]{1,0:T(8,128)(2,1)}, u32[]{:S(2)}) copy-start(bf16[64,2048]{1,0:T(8,128)(2,1)} %get-tuple-element.58) | copy-start | bytes 786436
  79.8 39.2 %copy-start.4 = (bf16[1,1,64,8192]{3,2,1,0:T(8,128)(2,1)S(1)}, bf16[1,1,64,8192]{3,2,1,0:T(8,128)(2,1)}, u32[]{:S(2)}) copy-start(bf16[1,1,64,8192]{3,2,1,0:T(8,128)(2,1)} %param.14) | copy-start | bytes 3145732
  85.9 27.7 %collective-permute-start.11 = (bf16[64,2048]{1,0:T(8,128)(2,1)}, bf16[64,2048]{1,0:T(8,128)(2,1)S(1)}, u32[]{:S(2)}, u32[]{:S(2)}) collective-permute-start(bf16[64,2048]{1,0:T(8,128)(2,1)} %get-tuple-element.43), channel_id=1, source_target_pairs={{0,1},{1,2},{2,3},{3,0},{4,5},{5,6},{6,7},{7,4},{8,9},{9,10},{10,1... | collective-permute-start | bytes 786440 | tf_op jit(solution)/shard_map/ppermute | solution.py:69
  91.8 6.2 %collective-permute-start.16 = (bf16[2,2,64,256]{3,2,0,1:T(8,128)(2,1)S(1)}, bf16[2,2,64,256]{3,2,0,1:T(8,128)(2,1)S(1)}, u32[]{:S(2)}, u32[]{:S(2)}) collective-permute-start(bf16[2,2,64,256]{3,2,0,1:T(8,128)(2,1)S(1)} %pad_maximum_fusion.5), channel_id=1, source_target_pairs={{0,3},{1,0},{2,1},{3,2},{4,7},{5,4},{6,5},{7,6},{8,11},{9,8},{10,9... | collective-permute-start | bytes 393224 | tf_op jit(solution)/shard_map/ppermute | solution.py:69
  93.9 15.9 %collective-permute-start.15 = (bf16[2,2,64,256]{3,2,0,1:T(8,128)(2,1)S(1)}, bf16[2,2,64,256]{3,2,0,1:T(8,128)(2,1)S(1)}, u32[]{:S(2)}, u32[]{:S(2)}) collective-permute-start(bf16[2,2,64,256]{3,2,0,1:T(8,128)(2,1)S(1)} %pad_maximum_fusion.5), channel_id=1, source_target_pairs={{0,2},{1,3},{2,0},{3,1},{4,6},{5,7},{6,4},{7,5},{8,10},{9,11},{10,... | collective-permute-start | bytes 393224 | tf_op jit(solution)/shard_map/ppermute | solution.py:69
  94.9 15.0 %collective-permute-start.14 = (bf16[2,2,64,256]{3,2,0,1:T(8,128)(2,1)S(1)}, bf16[2,2,64,256]{3,2,0,1:T(8,128)(2,1)S(1)}, u32[]{:S(2)}, u32[]{:S(2)}) collective-permute-start(bf16[2,2,64,256]{3,2,0,1:T(8,128)(2,1)S(1)} %pad_maximum_fusion.5), channel_id=1, source_target_pairs={{0,1},{1,2},{2,3},{3,0},{4,5},{5,6},{6,7},{7,4},{8,9},{9,10},{10,1... | collective-permute-start | bytes 393224 | tf_op jit(solution)/shard_map/ppermute | solution.py:69
  98.0 27.0 %collective-permute-start.12 = (bf16[64,2048]{1,0:T(8,128)(2,1)S(1)}, bf16[64,2048]{1,0:T(8,128)(2,1)S(1)}, u32[]{:S(2)}, u32[]{:S(2)}) collective-permute-start(bf16[64,2048]{1,0:T(8,128)(2,1)S(1)} %copy-done.17), channel_id=1, source_target_pairs={{0,2},{1,3},{2,0},{3,1},{4,6},{5,7},{6,4},{7,5},{8,10},{9,11},{10,... | collective-permute-start | bytes 786440 | tf_op jit(solution)/shard_map/ppermute | solution.py:69
  109.8 16.4 %collective-permute-start.13 = (bf16[64,2048]{1,0:T(8,128)(2,1)S(1)}, bf16[64,2048]{1,0:T(8,128)(2,1)S(1)}, u32[]{:S(2)}, u32[]{:S(2)}) collective-permute-start(bf16[64,2048]{1,0:T(8,128)(2,1)S(1)} %copy-done.16), channel_id=1, source_target_pairs={{0,3},{1,0},{2,1},{3,2},{4,7},{5,4},{6,5},{7,6},{8,11},{9,8},{10,9... | collective-permute-start | bytes 786440 | tf_op jit(solution)/shard_map/ppermute | solution.py:69
  109.9 18.2 %collective-permute-start.8 = (bf16[64,2048]{1,0:T(8,128)(2,1)S(1)}, bf16[64,2048]{1,0:T(8,128)(2,1)S(1)}, u32[]{:S(2)}, u32[]{:S(2)}) collective-permute-start(bf16[64,2048]{1,0:T(8,128)(2,1)S(1)} %copy-done.15), channel_id=1, source_target_pairs={{0,1},{1,2},{2,3},{3,0},{4,5},{5,6},{6,7},{7,4},{8,9},{9,10},{10,1... | collective-permute-start | bytes 786440 | tf_op jit(solution)/shard_map/ppermute | solution.py:69
  113.7 27.0 %collective-permute-start.9 = (bf16[64,2048]{1,0:T(8,128)(2,1)S(1)}, bf16[64,2048]{1,0:T(8,128)(2,1)S(1)}, u32[]{:S(2)}, u32[]{:S(2)}) collective-permute-start(bf16[64,2048]{1,0:T(8,128)(2,1)S(1)} %copy-done.14), channel_id=1, source_target_pairs={{0,2},{1,3},{2,0},{3,1},{4,6},{5,7},{6,4},{7,5},{8,10},{9,11},{10,... | collective-permute-start | bytes 786440 | tf_op jit(solution)/shard_map/ppermute | solution.py:69
  116.1 24.6 %collective-permute-start.10 = (bf16[64,2048]{1,0:T(8,128)(2,1)S(1)}, bf16[64,2048]{1,0:T(8,128)(2,1)S(1)}, u32[]{:S(2)}, u32[]{:S(2)}) collective-permute-start(bf16[64,2048]{1,0:T(8,128)(2,1)S(1)} %copy-done.13), channel_id=1, source_target_pairs={{0,3},{1,0},{2,1},{3,2},{4,7},{5,4},{6,5},{7,6},{8,11},{9,8},{10,9... | collective-permute-start | bytes 786440 | tf_op jit(solution)/shard_map/ppermute | solution.py:69
  119.0 21.8 %copy-start.6 = (bf16[64,2048]{1,0:T(8,128)(2,1)S(1)}, bf16[64,2048]{1,0:T(8,128)(2,1)}, u32[]{:S(2)}) copy-start(bf16[64,2048]{1,0:T(8,128)(2,1)} %get-tuple-element.67) | copy-start | bytes 786436
  119.0 21.8 %copy-start.7 = (bf16[64,2048]{1,0:T(8,128)(2,1)S(1)}, bf16[64,2048]{1,0:T(8,128)(2,1)}, u32[]{:S(2)}) copy-start(bf16[64,2048]{1,0:T(8,128)(2,1)} %get-tuple-element.68) | copy-start | bytes 786436
  125.0 28.3 %collective-permute-start.3 = (bf16[64,8192]{1,0:T(8,128)(2,1)}, bf16[64,8192]{1,0:T(8,128)(2,1)}, u32[]{:S(2)}, u32[]{:S(2)}) collective-permute-start(bf16[64,8192]{1,0:T(8,128)(2,1)} %fusion.26), channel_id=1, source_target_pairs={{8,0},{16,8},{24,16},{9,1},{17,9},{25,17},{10,2},{18,10},{26,18},{... | collective-permute-start | bytes 3145736 | tf_op jit(solution)/shard_map/ppermute | solution.py:14
  140.8 1.0 copy-start.11
  149.4 3.9 %copy-start.5 = (bf16[1,64,8192]{2,1,0:T(8,128)(2,1)S(1)}, bf16[1,64,8192]{2,1,0:T(8,128)(2,1)}, u32[]{:S(2)}) copy-start(bf16[1,64,8192]{2,1,0:T(8,128)(2,1)} %param.15) | copy-start | bytes 3145732
where the time goes:
time: 159 us; the launch traced here: 156 us
  waiting for transfers between devices  49.2 us (31%)
  starting transfers between devices  35.6 us (22%)
  matrix products  32.8 us (21%)
  other arithmetic  19.8 us (12%)
  local copies, waits for them, and re-layouts  17.7 us (11%)
    ppermute x16, waiting for transfers between devices, rotated(): lax.ppermute(value, axis, [(source, (source + steps) % count) for source...  49.2 us
    ppermute x16, starting transfers between devices, rotated(): lax.ppermute(value, axis, [(source, (source + steps) % count) for source...  34.4 us
    dot_general x4, matrix products, partial(): lax.dot_general(rows, weights, (((1,), (1,)), ((), ())), preferred_elemen...  17.2 us
    dot_general x3, matrix products, project(): jnp.dot(rows, weights, preferred_element_type=jnp.float32)  7.25 us
    unnamed x43, local copies, waits for them, and re-layouts  5.4 us
    dot_general x2, matrix products, contract(): lax.dot_general(left, right, (((0,), (0,)), ((), ())), preferred_element_...  3.88 us
    another operation x4, other arithmetic, on_device(): normed_local = jnp.stack(normed_ticks)  3.48 us
    dynamic_slice x4, local copies, waits for them, and re-layouts, on_device(): lax.dynamic_slice_in_dim(pair_grad, owner_start(-k), row_count, axis=0)  3.37 us
  transfers between devices with their start and end apart: 17, of which 8 were waited for; matrix products, arithmetic and copies ran while one was open for 39% of the time, Pallas kernels for 0%

commit v1 on v0

--- a/solution.py
+++ b/solution.py
@@ -125,19 +125,15 @@
     other_ticks = []
     sent = ()
     for tick in ticks:
-        gathered = after(arrived[tick], *sent)
-        columns = [
-            [column_block(rows, j) for rows in gathered] for j in range(dp_count)
-        ]
+        gathered = after(arrived[tick], sent)
+        columns = [[column_block(rows, j) for rows in gathered] for j in range(dp_count)]
         columns = lax.optimization_barrier(columns)
         if tick > 0:
             gathered = after(gathered, columns)
         pieces = [projected_own[tick]] + [project(rows, weights) for rows in gathered]
         projected = jnp.zeros((row_total, pair_width), jnp.bfloat16)
         for k, piece in enumerate(pieces):
-            projected = lax.dynamic_update_slice_in_dim(
-                projected, piece, owner_start(-k), axis=0
-            )
+            projected = lax.dynamic_update_slice_in_dim(projected, piece, owner_start(-k), axis=0)
         query_grad, pair_grad = head_grads(
             projected,
             queries[0, 0, tick],
@@ -155,10 +151,8 @@
         leaving = [partial(pair_grad, k) for k in range(1, tensor_count)]
         leaving = lax.optimization_barrier(leaving)
         received.append([rotated(value, "tensor", k + 1) for k, value in enumerate(leaving)])
-        sent = tuple(leaving)
-        query_grad, pair_grad = after((query_grad, pair_grad), *sent)
-        if tick == 0:
-            columns = after(columns, *sent)
+        sent = (tuple(leaving), columns)
+        query_grad, pair_grad = after((query_grad, pair_grad), sent)
         other_ticks.append(
             [columns[0]]
             + [[rotated(value, "dp", j) for value in columns[j]] for j in range(1, dp_count)]
@@ -174,8 +168,11 @@
             )
         )
 
-    pair_local = jnp.stack(pair_list, axis=1)
-    pair_all = [pair_local] + [rotated(pair_local, "dp", j) for j in range(1, dp_count)]
+    pair_local = [jnp.stack([pairs[k] for pairs in pair_list]) for k in range(tensor_count)]
+    pair_local = lax.optimization_barrier(pair_local)
+    pair_all = [pair_local] + [
+        [rotated(pairs, "dp", j) for pairs in pair_local] for j in range(1, dp_count)
+    ]
 
     def norm_back(tick, *earlier):
         normed_grad = kept[tick].astype(jnp.float32)
@@ -195,7 +192,7 @@
     incoming = jnp.where(is_last, loss_cotangent[0], incoming)
     residual_grad = (incoming.astype(jnp.float32) + norm_back(1, outgoing)).astype(jnp.bfloat16)
 
-    own_columns, other_ticks, pair_all = after((own_columns, other_ticks, pair_all), outgoing)
+    own_columns, other_ticks, pair_all = after((own_columns, other_ticks, pair_all), residual_grad)
 
     def contract(columns, pairs):
         left = jnp.concatenate([value.reshape(-1, block_width) for value in columns])
@@ -206,11 +203,14 @@
 
     weight_sum = contract(own_columns, [value[0] for value in pair_all])
     if tensor_count > 1:
-        others = [
-            jnp.stack([jnp.stack([other_ticks[tick][j][k] for tick in ticks]) for k in range(tensor_count - 1)])
-            for j in range(dp_count)
-        ]
-        weight_sum = weight_sum + contract(others, [value[1:] for value in pair_all])
+        for tick in ticks:
+            weight_sum = weight_sum + contract(
+                [jnp.concatenate(columns) for columns in other_ticks[tick]],
+                [
+                    jnp.concatenate([value[tick] for value in pairs[1:]])
+                    for pairs in pair_all
+                ],
+            )
     projection_grad = weight_sum.astype(jnp.bfloat16).reshape(1, -1, 1, 2, head_size)
     query_all = jnp.stack(query_list)[None, None]
     return (query_all, residual_grad[None, None], projection_grad)
@@ -235,4 +235,6 @@
     )
 
 
-    return jax.shard_map(on_device, mesh=mesh, in_specs=in_specs, out_specs=out_specs, check_vma=False)
+    return jax.shard_map(
+        on_device, mesh=mesh, in_specs=in_specs, out_specs=out_specs, check_vma=False
+    )

time: 159 us -> 175 us (1.10)
  waiting for transfers between devices: 49.2 us -> 61.3 us
  starting transfers between devices: 35.6 us -> 42.9 us
  other arithmetic: 19.8 us -> 15.3 us
  local copies, waits for them, and re-layouts: 17.7 us -> 20.7 us
  matrix products: 32.8 us -> 30.5 us
    ppermute x16 -> x19, waiting for transfers between devices: 49.2 us -> 61.3 us  [rotated(): lax.ppermute(value, axis, [(source, (source + steps) % count) for source...]
    ppermute x16 -> x19, starting transfers between devices: 34.4 us -> 41.6 us  [rotated(): lax.ppermute(value, axis, [(source, (source + steps) % count) for source...]
    dynamic_slice x4 -> x0, local copies, waits for them, and re-layouts: 3.37 us -> none  [on_device(): lax.dynamic_slice_in_dim(pair_grad, owner_start(-k), row_count, axis=0)]
    another operation x2 -> x4, local copies, waits for them, and re-layouts: 0.02 us -> 3.35 us  [the longest x2 3.33 us: on_device(): jnp.stack([lax.dynamic_slice_in_dim(pair_grad, owner_start(-k), row_count...]
    broadcast_in_dim x1 -> x0, other arithmetic: 3.2 us -> none  [on_device(): return (query_all, residual_grad[None, None], projection_grad)]
    dot_general x4, matrix products: 17.2 us -> 14.9 us  [partial(): lax.dot_general(rows, weights, (((1,), (1,)), ((), ())), preferred_elemen...]
    convert_element_type x0 -> x1, other arithmetic: none -> 1.97 us  [on_device(): (incoming.astype(jnp.float32) + norm_back(1, outgoing)).astype(jnp.bfloat16)]
    dynamic_slice x1 -> x2, local copies, waits for them, and re-layouts: 2.83 us -> 4.57 us  [column_block(): lax.dynamic_slice_in_dim(value, start, block_width, axis=value.ndim - 1)]
  transfers between devices with their start and end apart: 17 -> 20, of which waited for: 8 -> 10; matrix products, arithmetic and copies ran while one was open for 39% -> 32% of each run, Pallas kernels for 0% -> 0%
where the time goes in v1:
time: 175 us; the launch traced here: 172 us
  waiting for transfers between devices  61.3 us (35%)
  starting transfers between devices  42.9 us (25%)
  matrix products  30.5 us (17%)
  local copies, waits for them, and re-layouts  20.7 us (12%)
  other arithmetic  15.3 us (9%)
    ppermute x19, waiting for transfers between devices, rotated(): lax.ppermute(value, axis, [(source, (source + steps) % count) for source...  61.3 us
    ppermute x19, starting transfers between devices, rotated(): lax.ppermute(value, axis, [(source, (source + steps) % count) for source...  41.6 us
    dot_general x4, matrix products, partial(): lax.dot_general(rows, weights, (((1,), (1,)), ((), ())), preferred_elemen...  14.9 us
    dot_general x3, matrix products, project(): jnp.dot(rows, weights, preferred_element_type=jnp.float32)  7.25 us
    dynamic_slice x2, local copies, waits for them, and re-layouts, column_block(): lax.dynamic_slice_in_dim(value, start, block_width, axis=value.ndim - 1)  4.57 us
    unnamed x61, local copies, waits for them, and re-layouts  3.81 us
    another operation x4, other arithmetic, on_device(): normed_local = jnp.stack(normed_ticks)  3.51 us
  transfers between devices with their start and end apart: 20, of which 10 were waited for; matrix products, arithmetic and copies ran while one was open for 32% of the time, Pallas kernels for 0%

profile of v1, /device:TPU:0, one launch (start us, length us, event | category | flops | bytes accessed | tf_op | source)
XLA Modules:
  0.0 172.1 jit_solution(14235081020956029186)
XLA Ops:
  1.4 1.7 slice_bitcast_fusion.1
  3.4 1.3 fusion.18
  4.7 3.0 %collective-permute-start = (bf16[64,8192]{1,0:T(8,128)(2,1)}, bf16[64,8192]{1,0:T(8,128)(2,1)}, u32[]{:S(2)}, u32[]{:S(2)}) collective-permute-start(bf16[64,8192]{1,0:T(8,128)(2,1)} %fusion.18), channel_id=1, source_target_pairs={{0,4},{4,0},{1,5},{5,1},{2,6},{6,2},{3,7},{7,3},{8,12},{12,8},{9,1... | collective-permute-start | bytes 3145736 | tf_op jit(solution)/shard_map/ppermute | solution.py:69
  8.0 1.3 fusion.21
  10.0 1.4 fusion.108
  11.3 2.1 %collective-permute-start.5 = (bf16[2,64,2048]{2,1,0:T(8,128)(2,1)}, bf16[2,64,2048]{2,1,0:T(8,128)(2,1)}, u32[]{:S(2)}, u32[]{:S(2)}) collective-permute-start(bf16[2,64,2048]{2,1,0:T(8,128)(2,1)} %get-tuple-element.90), channel_id=1, source_target_pairs={{0,1},{1,2},{2,3},{3,0},{4,5},{5,6},{6,7},{7,4},{8,9},{9,10},{10,1... | collective-permute-start | bytes 1572872 | tf_op jit(solution)/shard_map/ppermute | solution.py:69
  13.4 2.6 %collective-permute-start.6 = (bf16[2,64,2048]{2,1,0:T(8,128)(2,1)}, bf16[2,64,2048]{2,1,0:T(8,128)(2,1)}, u32[]{:S(2)}, u32[]{:S(2)}) collective-permute-start(bf16[2,64,2048]{2,1,0:T(8,128)(2,1)} %get-tuple-element.91), channel_id=1, source_target_pairs={{0,2},{1,3},{2,0},{3,1},{4,6},{5,7},{6,4},{7,5},{8,10},{9,11},{10,... | collective-permute-start | bytes 1572872 | tf_op jit(solution)/shard_map/ppermute | solution.py:69
  16.0 1.3 collective-permute-start.7
  17.4 1.5 pad_maximum_fusion
  21.4 1.2 copy.58
  23.5 3.1 %fusion.68 = bf16[128,256]{1,0:T(8,128)(2,1)S(1)} fusion(bf16[128,8192]{1,0:T(8,128)(2,1)S(1)} %bitcast.298, bf16[1024,8,2,128]{3,2,1,0:T(2,128)(2,1)} %bitcast.277), kind=kOutput, calls=%fused_computation.100 | convolution fusion | flops 536903680 | bytes 6356992 | tf_op jit(solution)/shard_map/dot_general | solution.py:24
  26.6 5.4 %collective-permute-done = bf16[64,8192]{1,0:T(8,128)(2,1)} collective-permute-done((bf16[64,8192]{1,0:T(8,128)(2,1)}, bf16[64,8192]{1,0:T(8,128)(2,1)}, u32[]{:S(2)}, u32[]{:S(2)}) %collective-permute-start) | collective-permute-done | bytes 1048608 | tf_op jit(solution)/shard_map/ppermute | solution.py:69
  32.0 2.1 %fusion.86 = bf16[128,256]{1,0:T(8,128)(2,1)S(1)} fusion(bf16[128,256]{1,0:T(8,128)(2,1)S(1)} %slice_dynamic-update-slice_fusion.1, s32[]{:T(128)S(6)} %select_n.54, bf16[64,8192]{1,0:T(8,128)(2,1)} %collective-permute-done, bf16[1024,8,2,128]{3,2,1,0:T(2,128)(2,1)S(1)} %bitcast.281), kind=kOutput, calls=%fused_computation.114 | convolution fusion | flops 268451840 | bytes 5275652 | tf_op jit(solution)/shard_map/dot_general | solution.py:24
  35.9 4.6 %convolution_convert_fusion.3 = bf16[64,8192]{1,0:T(8,128)(2,1)} fusion(bf16[1024,8,2,128]{3,2,1,0:T(2,128)(2,1)} %bitcast.278, s32[]{:T(128)S(6)} %select_n.56, bf16[128,128]{0,1:T(8,128)(2,1)S(1)} %fusion.81, bf16[128,128]{0,1:T(8,128)(2,1)S(1)} %fusion.73), kind=kOutput, calls=%fused_computation.7 | convolution fusion | flops 269025280 | bytes 5308420 | tf_op jit(solution)/shard_map/dot_general | solution.py:147
  40.5 2.4 %constant_dynamic-slice_fusion.6 = (bf16[64,2048]{1,0:T(8,128)(2,1)}, bf16[64,2048]{1,0:T(8,128)(2,1)}, bf16[64,2048]{1,0:T(8,128)(2,1)}, bf16[64,2048]{1,0:T(8,128)(2,1)}) fusion(bf16[64,8192]{1,0:T(8,128)(2,1)} %collective-permute-done, s32[]{:T(128)S(6)} %select_n.60, s32[]{:T(128)S(6)} %select_n.59, s32[]{:T(128)S(6)} %select_n.58, s32[]{:T(128)S(6)} %select_n.57), kind=kLoop, calls=%fused_computation.216 | loop fusion | bytes 2097168 | tf_op jit(solution)/shard_map/dynamic_slice | solution.py:106
  42.9 10.7 %collective-permute-done.1 = bf16[64,8192]{1,0:T(8,128)(2,1)} collective-permute-done((bf16[64,8192]{1,0:T(8,128)(2,1)}, bf16[64,8192]{1,0:T(8,128)(2,1)}, u32[]{:S(2)}, u32[]{:S(2)}) %collective-permute-start.1) | collective-permute-done | bytes 1048608 | tf_op jit(solution)/shard_map/ppermute | solution.py:69
  53.7 2.2 %constant_dynamic-slice_fusion.2 = (bf16[64,2048]{1,0:T(8,128)(2,1)}, bf16[64,2048]{1,0:T(8,128)(2,1)}, bf16[64,2048]{1,0:T(8,128)(2,1)}, bf16[64,2048]{1,0:T(8,128)(2,1)}) fusion(bf16[64,8192]{1,0:T(8,128)(2,1)} %collective-permute-done.1, s32[]{:T(128)S(6)} %select_n.60, s32[]{:T(128)S(6)} %select_n.59, s32[]{:T(128)S(6)} %select_n.58, s32[]{:T(128)S(6)} %select_n.57), kind=kLoop, calls=%fused_computation.212 | loop fusion | bytes 2097168 | tf_op jit(solution)/shard_map/dynamic_slice | solution.py:106
  55.8 2.1 %fusion.83 = bf16[128,256]{1,0:T(8,128)(2,1)S(1)} fusion(bf16[128,256]{1,0:T(8,128)(2,1)S(1)} %slice_dynamic-update-slice_fusion, s32[]{:T(128)S(6)} %select_n.54, bf16[64,8192]{1,0:T(8,128)(2,1)} %collective-permute-done.1, bf16[1024,8,2,128]{3,2,1,0:T(2,128)(2,1)S(1)} %bitcast.282), kind=kOutput, calls=%fused_computation.113 | convolution fusion | flops 268451840 | bytes 5275652 | tf_op jit(solution)/shard_map/dot_general | solution.py:24
  58.9 1.8 %collective-permute-start.2 = (bf16[64,8192]{1,0:T(8,128)(2,1)}, bf16[64,8192]{1,0:T(8,128)(2,1)}, u32[]{:S(2)}, u32[]{:S(2)}) collective-permute-start(bf16[64,8192]{1,0:T(8,128)(2,1)} %convolution_convert_fusion.3), channel_id=1, source_target_pairs={{0,4},{4,0},{1,5},{5,1},{2,6},{6,2},{3,7},{7,3},{8,12},{12,8},{9,1... | collective-permute-start | bytes 3145736 | tf_op jit(solution)/shard_map/ppermute | solution.py:69
  61.2 4.7 %convolution_convert_fusion.2 = bf16[64,8192]{1,0:T(8,128)(2,1)} fusion(bf16[1024,8,2,128]{3,2,1,0:T(2,128)(2,1)} %bitcast.279, s32[]{:T(128)S(6)} %select_n.56, bf16[128,128]{0,1:T(8,128)(2,1)S(1)} %fusion.82, bf16[128,128]{0,1:T(8,128)(2,1)S(1)} %fusion.74), kind=kOutput, calls=%fused_computation.6 | convolution fusion | flops 269025280 | bytes 5308420 | tf_op jit(solution)/shard_map/dot_general | solution.py:147
  67.7 1.8 %copy.77 = bf16[128,1,1024]{2,0,1:T(8,128)(2,1)} copy(bf16[128,1,1024]{0,2,1:T(8,128)(2,1)} %bitcast.304) | data formatting | bytes 524288 | tf_op jit(solution)/shard_map/optimization_barrier | solution.py:73
  70.1 1.7 fusion.64
  71.8 1.1 copy.66
  72.9 1.6 dynamic-slice_bitcast_fusion
  74.7 1.7 dynamic-slice_bitcast_fusion.1
  76.4 1.5 copy.78
  77.9 7.4 %collective-permute-done.2 = bf16[64,8192]{1,0:T(8,128)(2,1)} collective-permute-done((bf16[64,8192]{1,0:T(8,128)(2,1)}, bf16[64,8192]{1,0:T(8,128)(2,1)}, u32[]{:S(2)}, u32[]{:S(2)}) %collective-permute-start.2) | collective-permute-done | bytes 1048608 | tf_op jit(solution)/shard_map/ppermute | solution.py:69
  85.3 4.1 %fusion.28 = (f32[64]{0:T(128)S(1)}, f32[64,8192]{1,0:T(8,128)S(1)}) fusion(bf16[64,8192]{1,0:T(8,128)(2,1)} %collective-permute-done.2, f32[8192]{0:T(1024)S(1)} %bitcast.288, bf16[1,1,2,64,8192]{4,3,2,1,0:T(8,128)(2,1)S(1)} %copy-done.3, bf16[64,256]{0,1:T(8,128)(2,1)} %get-tuple-element.115, bf16[1024,8,2,128]{3,2,1,0:T(2,128)(2,1)} %bitcast.280), kind=kOutput, calls=%fused_computation.50 | convolution fusion | flops 272629696 | bytes 8454400 | tf_op jit(solution)/shard_map/dot_general | solution.py:147
  89.5 2.3 %fusion.27 = bf16[64,8192]{1,0:T(8,128)(2,1)S(1)} fusion(f32[64,8192]{1,0:T(8,128)S(1)} %get-tuple-element.127, bf16[64,8192]{1,0:T(8,128)(2,1)} %collective-permute-done.2, bf16[1,1,64,8192]{3,2,1,0:T(8,128)(2,1)S(1)} %copy-done.8, f32[64]{0:T(128)S(1)} %broadcast_multiply_fusion.13, f32[8192]{0:T(1024)S(1)} %bitcast.289, f32[64]{0:T(128)S(1)} %add_rsqrt_fusion.1, ...), kind=kLoop, calls=%fused_computation.49 | loop fusion | flops 6815744 | bytes 6324736 | tf_op jit(solution)/shard_map/convert_element_type | solution.py:189
  91.7 1.3 collective-permute-start.3
  94.0 11.9 %collective-permute-done.4 = bf16[64,8192]{1,0:T(8,128)(2,1)S(1)} collective-permute-done((bf16[64,8192]{1,0:T(8,128)(2,1)}, bf16[64,8192]{1,0:T(8,128)(2,1)S(1)}, u32[]{:S(2)}, u32[]{:S(2)}) %collective-permute-start.4) | collective-permute-done | bytes 1048608 | tf_op jit(solution)/shard_map/ppermute | solution.py:69
  106.0 1.5 collective-permute-start.8
  107.5 1.6 collective-permute-start.14
  109.1 1.3 collective-permute-start.16
  110.4 1.5 collective-permute-start.15
  111.9 1.6 fusion.35
  113.5 5.0 %collective-permute-done.14 = bf16[2,64,256]{2,1,0:T(8,128)(2,1)S(1)} collective-permute-done((bf16[2,64,256]{2,1,0:T(8,128)(2,1)S(1)}, bf16[2,64,256]{2,1,0:T(8,128)(2,1)S(1)}, u32[]{:S(2)}, u32[]{:S(2)}) %collective-permute-start.14) | collective-permute-done | bytes 65568 | tf_op jit(solution)/shard_map/ppermute | solution.py:69
  118.4 3.8 %collective-permute-start.17 = (bf16[2,64,256]{1,2,0:T(8,128)(2,1)S(1)}, bf16[2,64,256]{1,2,0:T(8,128)(2,1)S(1)}, u32[]{:S(2)}, u32[]{:S(2)}) collective-permute-start(bf16[2,64,256]{1,2,0:T(8,128)(2,1)S(1)} %pad_maximum_fusion.1), channel_id=1, source_target_pairs={{0,2},{1,3},{2,0},{3,1},{4,6},{5,7},{6,4},{7,5},{8,10},{9,11},{10,... | collective-permute-start | bytes 196616 | tf_op jit(solution)/shard_map/ppermute | solution.py:69
  123.0 3.9 %collective-permute-start.19 = (bf16[2,64,256]{1,2,0:T(8,128)(2,1)S(1)}, bf16[2,64,256]{1,2,0:T(8,128)(2,1)S(1)}, u32[]{:S(2)}, u32[]{:S(2)}) collective-permute-start(bf16[2,64,256]{1,2,0:T(8,128)(2,1)S(1)} %pad_maximum_fusion.1), channel_id=1, source_target_pairs={{0,3},{1,0},{2,1},{3,2},{4,7},{5,4},{6,5},{7,6},{8,11},{9,8},{10,9... | collective-permute-start | bytes 196616 | tf_op jit(solution)/shard_map/ppermute | solution.py:69
  126.8 2.2 %collective-permute-done.17 = bf16[2,64,256]{1,2,0:T(8,128)(2,1)S(1)} collective-permute-done((bf16[2,64,256]{1,2,0:T(8,128)(2,1)S(1)}, bf16[2,64,256]{1,2,0:T(8,128)(2,1)S(1)}, u32[]{:S(2)}, u32[]{:S(2)}) %collective-permute-start.17) | collective-permute-done | bytes 65568 | tf_op jit(solution)/shard_map/ppermute | solution.py:69
  129.6 11.6 %collective-permute-start.10 = (bf16[64,2048]{1,0:T(8,128)(2,1)S(1)}, bf16[64,2048]{1,0:T(8,128)(2,1)S(1)}, u32[]{:S(2)}, u32[]{:S(2)}) collective-permute-start(bf16[64,2048]{1,0:T(8,128)(2,1)S(1)} %copy-done.16), channel_id=1, source_target_pairs={{0,3},{1,0},{2,1},{3,2},{4,7},{5,4},{6,5},{7,6},{8,11},{9,8},{10,9... | collective-permute-start | bytes 786440 | tf_op jit(solution)/shard_map/ppermute | solution.py:69
  141.7 1.5 collective-permute-start.12
  143.2 2.8 %collective-permute-start.13 = (bf16[64,2048]{1,0:T(8,128)(2,1)S(1)}, bf16[64,2048]{1,0:T(8,128)(2,1)S(1)}, u32[]{:S(2)}, u32[]{:S(2)}) collective-permute-start(bf16[64,2048]{1,0:T(8,128)(2,1)S(1)} %copy-done.15), channel_id=1, source_target_pairs={{0,3},{1,0},{2,1},{3,2},{4,7},{5,4},{6,5},{7,6},{8,11},{9,8},{10,9... | collective-permute-start | bytes 786440 | tf_op jit(solution)/shard_map/ppermute | solution.py:69
  146.1 2.0 %fusion.34 = bf16[64,8192]{1,0:T(8,128)(2,1)} fusion(f32[64,8192]{1,0:T(8,128)S(1)} %get-tuple-element.129, bf16[64,8192]{1,0:T(8,128)(2,1)S(1)} %collective-permute-done.4, bf16[64,8192]{1,0:T(8,128)(2,1)S(1)} %collective-permute-done.3, bf16[1,64,8192]{2,1,0:T(8,128)(2,1)S(1)} %copy-done.9, f32[64]{0:T(128)S(1)} %broadcast_multiply_fusion.12, ...), kind=kLoop, calls=%fused_computation.56 | loop fusion | flops 7340032 | bytes 7373313 | tf_op jit(solution)/shard_map/convert_element_type | solution.py:193
  149.1 3.4 %collective-permute-done.11 = bf16[64,2048]{1,0:T(8,128)(2,1)S(1)} collective-permute-done((bf16[64,2048]{1,0:T(8,128)(2,1)S(1)}, bf16[64,2048]{1,0:T(8,128)(2,1)S(1)}, u32[]{:S(2)}, u32[]{:S(2)}) %collective-permute-start.11) | collective-permute-done | bytes 262176 | tf_op jit(solution)/shard_map/ppermute | solution.py:69
  152.4 13.5 %collective-permute-done.12 = bf16[64,2048]{1,0:T(8,128)(2,1)S(1)} collective-permute-done((bf16[64,2048]{1,0:T(8,128)(2,1)S(1)}, bf16[64,2048]{1,0:T(8,128)(2,1)S(1)}, u32[]{:S(2)}, u32[]{:S(2)}) %collective-permute-start.12) | collective-permute-done | bytes 262176 | tf_op jit(solution)/shard_map/ppermute | solution.py:69
  168.0 2.1 %fusion.15 = bf16[2048,256]{0,1:T(8,128)(2,1)S(1)} fusion(f32[2048,256]{0,1:T(8,128)S(1)} %fusion.97, f32[2048,256]{0,1:T(8,128)S(1)} %fusion.89, bf16[128,2048]{1,0:T(8,128)(2,1)} %bitcast.49, bf16[128,2048]{1,0:T(8,128)(2,1)} %bitcast.48, bf16[128,2048]{1,0:T(8,128)(2,1)} %bitcast.47, bf16[128,2048]{1,0:T(8,128)(2,1)S(1)} %bitcast.309, ...), kind=kOutput, calls=%fused_computation.37 | convolution fusion | flops 547880960 | bytes 7602176 | tf_op jit(solution)/shard_map/dot_general | solution.py:200
  170.1 2.0 %copy.80 = bf16[1,2048,1,2,128]{4,3,2,1,0:T(2,128)(2,1)} copy(bf16[1,2048,1,2,128]{1,4,3,2,0:T(8,128)(2,1)S(1)} %bitcast.299) | data formatting | bytes 2097152
  (122 shorter events, 16.9 us)
Async XLA Ops:
  4.7 27.3 %collective-permute-start = (bf16[64,8192]{1,0:T(8,128)(2,1)}, bf16[64,8192]{1,0:T(8,128)(2,1)}, u32[]{:S(2)}, u32[]{:S(2)}) collective-permute-start(bf16[64,8192]{1,0:T(8,128)(2,1)} %fusion.18), channel_id=1, source_target_pairs={{0,4},{4,0},{1,5},{5,1},{2,6},{6,2},{3,7},{7,3},{8,12},{12,8},{9,1... | collective-permute-start | bytes 3145736 | tf_op jit(solution)/shard_map/ppermute | solution.py:69
  9.3 44.3 %collective-permute-start.1 = (bf16[64,8192]{1,0:T(8,128)(2,1)}, bf16[64,8192]{1,0:T(8,128)(2,1)}, u32[]{:S(2)}, u32[]{:S(2)}) collective-permute-start(bf16[64,8192]{1,0:T(8,128)(2,1)} %fusion.21), channel_id=1, source_target_pairs={{0,4},{4,0},{1,5},{5,1},{2,6},{6,2},{3,7},{7,3},{8,12},{12,8},{9,1... | collective-permute-start | bytes 3145736 | tf_op jit(solution)/shard_map/ppermute | solution.py:69
  11.3 96.2 %collective-permute-start.5 = (bf16[2,64,2048]{2,1,0:T(8,128)(2,1)}, bf16[2,64,2048]{2,1,0:T(8,128)(2,1)}, u32[]{:S(2)}, u32[]{:S(2)}) collective-permute-start(bf16[2,64,2048]{2,1,0:T(8,128)(2,1)} %get-tuple-element.90), channel_id=1, source_target_pairs={{0,1},{1,2},{2,3},{3,0},{4,5},{5,6},{6,7},{7,4},{8,9},{9,10},{10,1... | collective-permute-start | bytes 1572872 | tf_op jit(solution)/shard_map/ppermute | solution.py:69
  13.4 95.7 %collective-permute-start.6 = (bf16[2,64,2048]{2,1,0:T(8,128)(2,1)}, bf16[2,64,2048]{2,1,0:T(8,128)(2,1)}, u32[]{:S(2)}, u32[]{:S(2)}) collective-permute-start(bf16[2,64,2048]{2,1,0:T(8,128)(2,1)} %get-tuple-element.91), channel_id=1, source_target_pairs={{0,2},{1,3},{2,0},{3,1},{4,6},{5,7},{6,4},{7,5},{8,10},{9,11},{10,... | collective-permute-start | bytes 1572872 | tf_op jit(solution)/shard_map/ppermute | solution.py:69
  16.0 2.9 %copy-start.10 = (bf16[1,1,2,128,1,1024]{5,3,4,2,1,0:T(8,128)(2,1)S(1)}, bf16[1,1,2,128,1,1024]{5,3,4,2,1,0:T(8,128)(2,1)}, u32[]{:S(2)}) copy-start(bf16[1,1,2,128,1,1024]{5,3,4,2,1,0:T(8,128)(2,1)} %param.12) | copy-start | bytes 1572868
  16.0 2.9 %copy-start.28 = (s32[1,1,2,128]{3,2,1,0:T(2,128)S(1)}, s32[1,1,2,128]{3,2,1,0:T(2,128)}, u32[]{:S(2)}) copy-start(s32[1,1,2,128]{3,2,1,0:T(2,128)} %param.17) | copy-start | bytes 3076
  16.0 3.1 %copy-start.11 = (bf16[1,1,2,128,1,1024]{5,3,4,2,1,0:T(8,128)(2,1)S(1)}, bf16[1,1,2,128,1,1024]{5,3,4,2,1,0:T(8,128)(2,1)}, u32[]{:S(2)}) copy-start(bf16[1,1,2,128,1,1024]{5,3,4,2,1,0:T(8,128)(2,1)} %param.13) | copy-start | bytes 1572868
  16.0 94.3 %collective-permute-start.7 = (bf16[2,64,2048]{2,1,0:T(8,128)(2,1)}, bf16[2,64,2048]{2,1,0:T(8,128)(2,1)}, u32[]{:S(2)}, u32[]{:S(2)}) collective-permute-start(bf16[2,64,2048]{2,1,0:T(8,128)(2,1)} %get-tuple-element.88), channel_id=1, source_target_pairs={{0,3},{1,0},{2,1},{3,2},{4,7},{5,4},{6,5},{7,6},{8,11},{9,8},{10,9... | collective-permute-start | bytes 1572872 | tf_op jit(solution)/shard_map/ppermute | solution.py:69
  18.9 1.0 copy-start.27
  18.9 4.6 %copy-start.4 = (bf16[2,64,8192]{2,1,0:T(8,128)(2,1)S(1)}, bf16[2,64,8192]{2,1,0:T(8,128)(2,1)}, u32[]{:S(2)}) copy-start(bf16[2,64,8192]{2,1,0:T(8,128)(2,1)} %pad_maximum_fusion) | copy-start | bytes 6291460
  21.4 12.7 %copy-start.5 = (bf16[1,1,1,128,1,1024]{3,5,4,2,1,0:T(8,128)(2,1)}, bf16[1,1,1,128,1,1024]{3,5,4,2,1,0:T(8,128)(2,1)S(1)}, u32[]{:S(2)}) copy-start(bf16[1,1,1,128,1,1024]{3,5,4,2,1,0:T(8,128)(2,1)S(1)} %copy.101) | copy-start | bytes 786436
  23.5 8.5 %copy-start = (bf16[1,8192,1,2,128]{4,3,2,1,0:T(2,128)(2,1)S(1)}, bf16[1,8192,1,2,128]{4,3,2,1,0:T(2,128)(2,1)}, u32[]{:S(2)}) copy-start(bf16[1,8192,1,2,128]{4,3,2,1,0:T(2,128)(2,1)} %param.11) | copy-start | bytes 12582916
  34.5 1.0 copy-start.6
  40.5 15.3 %copy-start.1 = (bf16[1,8192,1,2,128]{4,3,2,1,0:T(2,128)(2,1)S(1)}, bf16[1,8192,1,2,128]{4,3,2,1,0:T(2,128)(2,1)}, u32[]{:S(2)}) copy-start(bf16[1,8192,1,2,128]{4,3,2,1,0:T(2,128)(2,1)} %param.11) | copy-start | bytes 12582916
  58.0 3.0 %copy-start.22 = (bf16[128,256]{1,0:T(8,128)(2,1)}, bf16[128,256]{1,0:T(8,128)(2,1)S(1)}, u32[]{:S(2)}) copy-start(bf16[128,256]{1,0:T(8,128)(2,1)S(1)} %fusion.83) | copy-start | bytes 196612
  58.9 26.4 %collective-permute-start.2 = (bf16[64,8192]{1,0:T(8,128)(2,1)}, bf16[64,8192]{1,0:T(8,128)(2,1)}, u32[]{:S(2)}, u32[]{:S(2)}) collective-permute-start(bf16[64,8192]{1,0:T(8,128)(2,1)} %convolution_convert_fusion.3), channel_id=1, source_target_pairs={{0,4},{4,0},{1,5},{5,1},{2,6},{6,2},{3,7},{7,3},{8,12},{12,8},{9,1... | collective-permute-start | bytes 3145736 | tf_op jit(solution)/shard_map/ppermute | solution.py:69
  61.2 5.6 %copy-start.23 = (bf16[128,256]{1,0:T(8,128)(2,1)S(1)}, bf16[128,256]{1,0:T(8,128)(2,1)}, u32[]{:S(2)}) copy-start(bf16[128,256]{1,0:T(8,128)(2,1)} %copy-done.22) | copy-start | bytes 196612
  65.8 19.5 %copy-start.3 = (bf16[1,1,2,64,8192]{4,3,2,1,0:T(8,128)(2,1)S(1)}, bf16[1,1,2,64,8192]{4,3,2,1,0:T(8,128)(2,1)}, u32[]{:S(2)}) copy-start(bf16[1,1,2,64,8192]{4,3,2,1,0:T(8,128)(2,1)} %param.9) | copy-start | bytes 6291460
  65.9 40.1 %collective-permute-start.4 = (bf16[64,8192]{1,0:T(8,128)(2,1)}, bf16[64,8192]{1,0:T(8,128)(2,1)S(1)}, u32[]{:S(2)}, u32[]{:S(2)}) collective-permute-start(bf16[64,8192]{1,0:T(8,128)(2,1)} %convolution_convert_fusion.2), channel_id=1, source_target_pairs={{0,4},{4,0},{1,5},{5,1},{2,6},{6,2},{3,7},{7,3},{8,12},{12,8},{9,1... | collective-permute-start | bytes 3145736 | tf_op jit(solution)/shard_map/ppermute | solution.py:69
  77.9 11.5 %copy-start.8 = (bf16[1,1,64,8192]{3,2,1,0:T(8,128)(2,1)S(1)}, bf16[1,1,64,8192]{3,2,1,0:T(8,128)(2,1)}, u32[]{:S(2)}) copy-start(bf16[1,1,64,8192]{3,2,1,0:T(8,128)(2,1)} %param.14) | copy-start | bytes 3145732
  89.4 3.6 %copy-start.26 = (bf16[64,256]{1,0:T(8,128)(2,1)S(1)}, bf16[64,256]{1,0:T(8,128)(2,1)}, u32[]{:S(2)}) copy-start(bf16[64,256]{1,0:T(8,128)(2,1)} %copy.78) | copy-start | bytes 98308
  89.4 3.6 %copy-start.24 = (bf16[1,64,256]{1,2,0:T(8,128)(2,1)S(1)}, bf16[1,64,256]{1,2,0:T(8,128)(2,1)}, u32[]{:S(2)}) copy-start(bf16[1,64,256]{1,2,0:T(8,128)(2,1)} %get-tuple-element.116) | copy-start | bytes 98308
  89.4 3.6 %copy-start.25 = (bf16[1,64,256]{1,2,0:T(8,128)(2,1)S(1)}, bf16[1,64,256]{1,2,0:T(8,128)(2,1)}, u32[]{:S(2)}) copy-start(bf16[1,64,256]{1,2,0:T(8,128)(2,1)} %get-tuple-element.114) | copy-start | bytes 98308
  89.4 3.7 %copy-start.7 = (bf16[128,1,1024]{2,0,1:T(8,128)(2,1)S(1)}, bf16[128,1,1024]{2,0,1:T(8,128)(2,1)}, u32[]{:S(2)}) copy-start(bf16[128,1,1024]{2,0,1:T(8,128)(2,1)} %copy.77) | copy-start | bytes 786436
  89.4 16.5 %copy-start.20 = (bf16[64,2048]{1,0:T(8,128)(2,1)S(1)}, bf16[64,2048]{1,0:T(8,128)(2,1)}, u32[]{:S(2)}) copy-start(bf16[64,2048]{1,0:T(8,128)(2,1)} %get-tuple-element.43) | copy-start | bytes 786436
  89.5 22.4 %copy-start.2 = (bf16[1,8192,1,2,128]{4,3,2,1,0:T(2,128)(2,1)S(1)}, bf16[1,8192,1,2,128]{4,3,2,1,0:T(2,128)(2,1)}, u32[]{:S(2)}) copy-start(bf16[1,8192,1,2,128]{4,3,2,1,0:T(2,128)(2,1)} %param.11) | copy-start | bytes 12582916
  91.7 51.5 %collective-permute-start.3 = (bf16[64,8192]{1,0:T(8,128)(2,1)S(1)}, bf16[64,8192]{1,0:T(8,128)(2,1)S(1)}, u32[]{:S(2)}, u32[]{:S(2)}) collective-permute-start(bf16[64,8192]{1,0:T(8,128)(2,1)S(1)} %fusion.27), channel_id=1, source_target_pairs={{8,0},{16,8},{24,16},{9,1},{17,9},{25,17},{10,2},{18,10},{26,18},{... | collective-permute-start | bytes 3145736 | tf_op jit(solution)/shard_map/ppermute | solution.py:14
  94.0 35.1 %copy-start.18 = (bf16[64,2048]{1,0:T(8,128)(2,1)S(1)}, bf16[64,2048]{1,0:T(8,128)(2,1)}, u32[]{:S(2)}) copy-start(bf16[64,2048]{1,0:T(8,128)(2,1)} %get-tuple-element.44) | copy-start | bytes 786436
  94.0 35.6 %copy-start.16 = (bf16[64,2048]{1,0:T(8,128)(2,1)S(1)}, bf16[64,2048]{1,0:T(8,128)(2,1)}, u32[]{:S(2)}) copy-start(bf16[64,2048]{1,0:T(8,128)(2,1)} %get-tuple-element.45) | copy-start | bytes 786436
  94.0 47.2 %copy-start.19 = (bf16[64,2048]{1,0:T(8,128)(2,1)S(1)}, bf16[64,2048]{1,0:T(8,128)(2,1)}, u32[]{:S(2)}) copy-start(bf16[64,2048]{1,0:T(8,128)(2,1)} %get-tuple-element.49) | copy-start | bytes 786436
  94.0 47.7 %copy-start.17 = (bf16[64,2048]{1,0:T(8,128)(2,1)S(1)}, bf16[64,2048]{1,0:T(8,128)(2,1)}, u32[]{:S(2)}) copy-start(bf16[64,2048]{1,0:T(8,128)(2,1)} %get-tuple-element.50) | copy-start | bytes 786436
  94.0 49.2 %copy-start.15 = (bf16[64,2048]{1,0:T(8,128)(2,1)S(1)}, bf16[64,2048]{1,0:T(8,128)(2,1)}, u32[]{:S(2)}) copy-start(bf16[64,2048]{1,0:T(8,128)(2,1)} %get-tuple-element.51) | copy-start | bytes 786436
  94.0 52.1 %copy-start.9 = (bf16[1,64,8192]{2,1,0:T(8,128)(2,1)S(1)}, bf16[1,64,8192]{2,1,0:T(8,128)(2,1)}, u32[]{:S(2)}) copy-start(bf16[1,64,8192]{2,1,0:T(8,128)(2,1)} %param.15) | copy-start | bytes 3145732
  106.0 35.8 %collective-permute-start.8 = (bf16[64,2048]{1,0:T(8,128)(2,1)S(1)}, bf16[64,2048]{1,0:T(8,128)(2,1)S(1)}, u32[]{:S(2)}, u32[]{:S(2)}) collective-permute-start(bf16[64,2048]{1,0:T(8,128)(2,1)S(1)} %copy-done.20), channel_id=1, source_target_pairs={{0,1},{1,2},{2,3},{3,0},{4,5},{5,6},{6,7},{7,4},{8,9},{9,10},{10,1... | collective-permute-start | bytes 786440 | tf_op jit(solution)/shard_map/ppermute | solution.py:69
  107.5 10.9 %collective-permute-start.14 = (bf16[2,64,256]{2,1,0:T(8,128)(2,1)S(1)}, bf16[2,64,256]{2,1,0:T(8,128)(2,1)S(1)}, u32[]{:S(2)}, u32[]{:S(2)}) collective-permute-start(bf16[2,64,256]{2,1,0:T(8,128)(2,1)S(1)} %pad_maximum_fusion.4), channel_id=1, source_target_pairs={{0,1},{1,2},{2,3},{3,0},{4,5},{5,6},{6,7},{7,4},{8,9},{9,10},{10,1... | collective-permute-start | bytes 196616 | tf_op jit(solution)/shard_map/ppermute | solution.py:69
  109.1 13.9 %collective-permute-start.16 = (bf16[2,64,256]{2,1,0:T(8,128)(2,1)S(1)}, bf16[2,64,256]{2,1,0:T(8,128)(2,1)S(1)}, u32[]{:S(2)}, u32[]{:S(2)}) collective-permute-start(bf16[2,64,256]{2,1,0:T(8,128)(2,1)S(1)} %pad_maximum_fusion.4), channel_id=1, source_target_pairs={{0,2},{1,3},{2,0},{3,1},{4,6},{5,7},{6,4},{7,5},{8,10},{9,11},{10,... | collective-permute-start | bytes 196616 | tf_op jit(solution)/shard_map/ppermute | solution.py:69
  110.4 11.8 %collective-permute-start.15 = (bf16[2,64,256]{1,2,0:T(8,128)(2,1)S(1)}, bf16[2,64,256]{1,2,0:T(8,128)(2,1)S(1)}, u32[]{:S(2)}, u32[]{:S(2)}) collective-permute-start(bf16[2,64,256]{1,2,0:T(8,128)(2,1)S(1)} %pad_maximum_fusion.1), channel_id=1, source_target_pairs={{0,1},{1,2},{2,3},{3,0},{4,5},{5,6},{6,7},{7,4},{8,9},{9,10},{10,1... | collective-permute-start | bytes 196616 | tf_op jit(solution)/shard_map/ppermute | solution.py:69
  118.4 10.6 %collective-permute-start.17 = (bf16[2,64,256]{1,2,0:T(8,128)(2,1)S(1)}, bf16[2,64,256]{1,2,0:T(8,128)(2,1)S(1)}, u32[]{:S(2)}, u32[]{:S(2)}) collective-permute-start(bf16[2,64,256]{1,2,0:T(8,128)(2,1)S(1)} %pad_maximum_fusion.1), channel_id=1, source_target_pairs={{0,2},{1,3},{2,0},{3,1},{4,6},{5,7},{6,4},{7,5},{8,10},{9,11},{10,... | collective-permute-start | bytes 196616 | tf_op jit(solution)/shard_map/ppermute | solution.py:69
  122.2 7.4 %collective-permute-start.18 = (bf16[2,64,256]{2,1,0:T(8,128)(2,1)S(1)}, bf16[2,64,256]{2,1,0:T(8,128)(2,1)S(1)}, u32[]{:S(2)}, u32[]{:S(2)}) collective-permute-start(bf16[2,64,256]{2,1,0:T(8,128)(2,1)S(1)} %pad_maximum_fusion.4), channel_id=1, source_target_pairs={{0,3},{1,0},{2,1},{3,2},{4,7},{5,4},{6,5},{7,6},{8,11},{9,8},{10,9... | collective-permute-start | bytes 196616 | tf_op jit(solution)/shard_map/ppermute | solution.py:69
  123.0 18.2 %collective-permute-start.19 = (bf16[2,64,256]{1,2,0:T(8,128)(2,1)S(1)}, bf16[2,64,256]{1,2,0:T(8,128)(2,1)S(1)}, u32[]{:S(2)}, u32[]{:S(2)}) collective-permute-start(bf16[2,64,256]{1,2,0:T(8,128)(2,1)S(1)} %pad_maximum_fusion.1), channel_id=1, source_target_pairs={{0,3},{1,0},{2,1},{3,2},{4,7},{5,4},{6,5},{7,6},{8,11},{9,8},{10,9... | collective-permute-start | bytes 196616 | tf_op jit(solution)/shard_map/ppermute | solution.py:69
  129.0 20.0 %collective-permute-start.9 = (bf16[64,2048]{1,0:T(8,128)(2,1)S(1)}, bf16[64,2048]{1,0:T(8,128)(2,1)S(1)}, u32[]{:S(2)}, u32[]{:S(2)}) collective-permute-start(bf16[64,2048]{1,0:T(8,128)(2,1)S(1)} %copy-done.18), channel_id=1, source_target_pairs={{0,2},{1,3},{2,0},{3,1},{4,6},{5,7},{6,4},{7,5},{8,10},{9,11},{10,... | collective-permute-start | bytes 786440 | tf_op jit(solution)/shard_map/ppermute | solution.py:69
  129.6 19.5 %collective-permute-start.10 = (bf16[64,2048]{1,0:T(8,128)(2,1)S(1)}, bf16[64,2048]{1,0:T(8,128)(2,1)S(1)}, u32[]{:S(2)}, u32[]{:S(2)}) collective-permute-start(bf16[64,2048]{1,0:T(8,128)(2,1)S(1)} %copy-done.16), channel_id=1, source_target_pairs={{0,3},{1,0},{2,1},{3,2},{4,7},{5,4},{6,5},{7,6},{8,11},{9,8},{10,9... | collective-permute-start | bytes 786440 | tf_op jit(solution)/shard_map/ppermute | solution.py:69
  141.1 11.3 %collective-permute-start.11 = (bf16[64,2048]{1,0:T(8,128)(2,1)S(1)}, bf16[64,2048]{1,0:T(8,128)(2,1)S(1)}, u32[]{:S(2)}, u32[]{:S(2)}) collective-permute-start(bf16[64,2048]{1,0:T(8,128)(2,1)S(1)} %copy-done.19), channel_id=1, source_target_pairs={{0,1},{1,2},{2,3},{3,0},{4,5},{5,6},{6,7},{7,4},{8,9},{9,10},{10,1... | collective-permute-start | bytes 786440 | tf_op jit(solution)/shard_map/ppermute | solution.py:69
  141.7 24.2 %collective-permute-start.12 = (bf16[64,2048]{1,0:T(8,128)(2,1)S(1)}, bf16[64,2048]{1,0:T(8,128)(2,1)S(1)}, u32[]{:S(2)}, u32[]{:S(2)}) collective-permute-start(bf16[64,2048]{1,0:T(8,128)(2,1)S(1)} %copy-done.17), channel_id=1, source_target_pairs={{0,2},{1,3},{2,0},{3,1},{4,6},{5,7},{6,4},{7,5},{8,10},{9,11},{10,... | collective-permute-start | bytes 786440 | tf_op jit(solution)/shard_map/ppermute | solution.py:69
  143.2 22.7 %collective-permute-start.13 = (bf16[64,2048]{1,0:T(8,128)(2,1)S(1)}, bf16[64,2048]{1,0:T(8,128)(2,1)S(1)}, u32[]{:S(2)}, u32[]{:S(2)}) collective-permute-start(bf16[64,2048]{1,0:T(8,128)(2,1)S(1)} %copy-done.15), channel_id=1, source_target_pairs={{0,3},{1,0},{2,1},{3,2},{4,7},{5,4},{6,5},{7,6},{8,11},{9,8},{10,9... | collective-permute-start | bytes 786440 | tf_op jit(solution)/shard_map/ppermute | solution.py:69
  146.0 19.9 %copy-start.14 = (bf16[64,2048]{1,0:T(8,128)(2,1)S(1)}, bf16[64,2048]{1,0:T(8,128)(2,1)}, u32[]{:S(2)}) copy-start(bf16[64,2048]{1,0:T(8,128)(2,1)} %get-tuple-element.75) | copy-start | bytes 786436
  166.0 1.0 copy-start.13
  166.9 1.0 copy-start.12
  (1 other events, 0.9 us)
